TPU v7x, 128 devices: a whole 4x4x4 slice. The times are simulated.
128 devices in a mesh: dp: 4 (over x), cp: 32 (over z, y, core).
Axes of the slice: x: 4, y: 4, z: 4, core: 2. Of those that a mesh axis runs over, the one named last changes fastest.
Arguments:
- tokens: bfloat16 [4, 4096, 4096], P('dp', 'cp'), may hold values from -60 to 60
- qkv_weight: bfloat16 [4096, 3072], replicated, may hold values from -0.09375 to 0.09375
- owner_slot: int32 [4, 32], P('dp', 'cp'), may hold values from 0 to 3, as said below
- slab_sequence: int32 [4, 32], replicated, may hold values from 0 to 16, as said below
- slab_order: int32 [4, 32], replicated, may hold values from 0 to 15, as said below
Outputs:
- context: bfloat16 [4, 4096, 2048], P('dp', 'cp')
Inputs may be any that keep to these rules, and one draw needn't show every extreme that they name: For every column c, the entries owner_slot[a, c] over all rows a are 0 to 3, each once. `slab_sequence`: in each row, the slabs with one sequence number carry the orders 0 to L-1, each once, L being their count; no sequence has more than 16 slabs. `slab_order`: see slab_sequence.
All inputs are finite; a program needn't handle non-finite values.
Results may differ from a plain program's by a relative error of at most 0.006.
The roundings to bfloat16 on the way count: a program that leaves them out, or rounds other values in their place, can miss the bound.
Values may be sent and summed in bfloat16 or wider, within the bound.
A program may use at most 128 MiB of HBM per device.

v0:
```python
import jax
import jax.numpy as jnp
from jax import lax
from jax.sharding import PartitionSpec as P

QH = 16
KVH = 4
HD = 128


ROPE_BASE = 500000.0
NEG_FILL = -1e30


def rotate(heads, positions):
    half_dim = heads.shape[-1] // 2
    frequency = ROPE_BASE ** (-jnp.arange(half_dim, dtype=jnp.float32) * 2.0 / heads.shape[-1])
    angles = positions.astype(jnp.float32)[:, None] * frequency[None, :]
    cosine = jnp.cos(angles)[:, None, :]
    sine_part = jnp.sin(angles)[:, None, :]
    first_half = heads[..., :half_dim]
    second_half = heads[..., half_dim:]
    return jnp.concatenate(
        [
            first_half * cosine - second_half * sine_part,
            second_half * cosine + first_half * sine_part,
        ],
        axis=-1,
    )


def project(input_rows, weight, positions):
    projected = jnp.dot(input_rows, weight, preferred_element_type=jnp.float32)
    count_rows = input_rows.shape[0]
    query = rotate(projected[:, : QH * HD].reshape(count_rows, QH, HD), positions).astype(
        jnp.bfloat16
    )
    key_heads = rotate(
        projected[:, QH * HD : (QH + KVH) * HD].reshape(count_rows, KVH, HD), positions
    ).astype(jnp.bfloat16)
    value_heads = projected[:, (QH + KVH) * HD :].astype(jnp.bfloat16)
    key_value = jnp.concatenate([key_heads.reshape(count_rows, KVH * HD), value_heads], axis=1)
    return (query.reshape(count_rows, QH * HD), key_value)


def local(tokens, qkv_weight, owner_slot, slab_sequence, slab_order):
    loader_rows = tokens[0]
    local_targets = owner_slot[0]
    slab_count = local_targets.shape[0]
    tok_dev = loader_rows.shape[0]
    slab_len = tok_dev // slab_count
    groups_count = lax.axis_size("dp")
    my_row = lax.axis_index("dp")
    column = lax.axis_index("cp")
    row_slabs = slab_sequence.shape[1]
    row_tok = row_slabs * slab_len
    group_size = QH // KVH
    offsets = jnp.arange(slab_len, dtype=jnp.int32)
    destinations = jnp.arange(groups_count * slab_count, dtype=jnp.int32)
    selector = (local_targets[None, :] == destinations[:, None]).astype(jnp.bfloat16)
    own_order = lax.dynamic_slice(slab_order, (my_row, column * slab_count), (1, slab_count))[0]
    own_pos = (own_order[:, None] * slab_len + offsets[None, :]).reshape(tok_dev)
    sent_row = local_targets // slab_count
    sent_slab = column * slab_count + local_targets % slab_count
    sent_order = slab_order[sent_row, sent_slab]
    sent_pos = (sent_order[:, None] * slab_len + offsets[None, :]).reshape(tok_dev)
    query_local, key_value_local = project(loader_rows, qkv_weight, sent_pos)
    combined = jnp.concatenate([query_local, key_value_local], axis=1)
    col_width = combined.shape[1]
    packed = jnp.einsum(
        "pj,jtd->ptd",
        selector,
        combined.reshape(slab_count, slab_len, col_width),
        preferred_element_type=jnp.float32,
    )
    received = lax.all_to_all(
        packed.astype(jnp.bfloat16).reshape(groups_count * slab_count * slab_len, col_width),
        "dp",
        split_axis=0,
        concat_axis=0,
        tiled=True,
    )
    unpack_col_width = received.shape[1]
    received = jnp.sum(
        received.reshape(groups_count, tok_dev, unpack_col_width), axis=0, dtype=jnp.float32
    ).astype(jnp.bfloat16)
    query = received[:, : QH * HD]
    key_value = received[:, QH * HD :]
    row_sequence = lax.dynamic_index_in_dim(slab_sequence, my_row, 0, keepdims=False)
    row_order = lax.dynamic_index_in_dim(slab_order, my_row, 0, keepdims=False)
    code_row = (
        row_sequence[:, None] * row_tok + row_order[:, None] * slab_len + offsets[None, :]
    ).reshape(row_tok)
    query_code = lax.dynamic_slice_in_dim(code_row, column * tok_dev, tok_dev)
    seq_start = query_code - own_pos
    query_groups = query.reshape(tok_dev, KVH, group_size, HD)
    score_scale = HD ** (-0.5)

    def update(state_now, block_keys, key_code):
        row_peak, denom_sum, weighted = state_now
        block_rows = block_keys.shape[0]
        allowed = (key_code[None, :] <= query_code[:, None]) & (
            key_code[None, :] >= seq_start[:, None]
        )

        def compute(state_in):
            peak_in, denom_in, weighted_in = state_in
            key_part = block_keys[:, : KVH * HD].reshape(block_rows, KVH, HD)
            value_part = block_keys[:, KVH * HD :].reshape(block_rows, KVH, HD)
            scores = (
                jnp.einsum(
                    "tgjh,ngh->gjtn", query_groups, key_part, preferred_element_type=jnp.float32
                )
                * score_scale
            )
            scores = jnp.where(allowed, scores, NEG_FILL)
            new_peak = jnp.maximum(peak_in, jnp.max(scores, axis=-1))
            weights = jnp.where(allowed, jnp.exp(scores - new_peak[..., None]), 0.0)
            rescale = jnp.exp(peak_in - new_peak)
            denom_out = denom_in * rescale + jnp.sum(weights, axis=-1)
            product = jnp.einsum(
                "gjtn,ngh->gjth",
                weights.astype(jnp.bfloat16),
                value_part,
                preferred_element_type=jnp.float32,
            )
            return (new_peak, denom_out, weighted_in * rescale[..., None] + product)

        return lax.cond(
            jnp.any(allowed), compute, lambda state_in: state_in, (row_peak, denom_sum, weighted)
        )

    start_state = (
        jnp.full((KVH, group_size, tok_dev), NEG_FILL, jnp.float32),
        jnp.zeros((KVH, group_size, tok_dev), jnp.float32),
        jnp.zeros((KVH, group_size, tok_dev, HD), jnp.float32),
    )
    shard_rows = lax.all_gather(key_value, "cp", axis=0, tiled=True)
    count_keys = shard_rows.shape[0]
    key_code = code_row
    step_rows = 1024
    steps_count = count_keys // step_rows

    def scan_step(state_in, pieces):
        return (update(state_in, pieces[0], pieces[1]), None)

    state_out, unused = lax.scan(
        scan_step,
        start_state,
        (
            shard_rows.reshape(steps_count, step_rows, shard_rows.shape[1]),
            key_code.reshape(steps_count, step_rows),
        ),
    )
    row_peak, denom_sum, weighted = state_out
    context = (weighted / denom_sum[..., None]).transpose(2, 0, 1, 3).reshape(tok_dev, QH * HD)
    return context.astype(jnp.bfloat16)[None]


def solution(mesh):
    in_specs = (P("dp", "cp", None), P(), P("dp", "cp"), P(), P())
    out_specs = P("dp", "cp", None)
    return jax.shard_map(local, mesh=mesh, in_specs=in_specs, out_specs=out_specs, check_vma=False)
```

profile of v0, /device:TPU:7, one launch (start us, length us, event | category | flops | bytes accessed | tf_op | source)
XLA Modules:
  0.0 182.6 jit_solution(14069714040307647107)
XLA Ops:
  7.8 10.0 %fusion.13 = f32[128,3072]{1,0:T(8,128)S(1)} fusion(bf16[4096,3072]{1,0:T(8,128)(2,1)} %param.10, bf16[1,128,4096]{2,1,0:T(8,128)(2,1)S(1)} %copy-done), kind=kOutput, calls=%fused_computation.19 | convolution fusion | flops 3221225472 | bytes 27787264 | tf_op jit(solution)/shard_map/dot_general | solution.py:33
  22.6 39.0 %all_to_all.6 = bf16[4,128,3072]{2,1,0:T(8,128)(2,1)} all-to-all(bf16[4,128,3072]{2,1,0:T(8,128)(2,1)S(1)} %multiply_convert_fusion), channel_id=1, replica_groups=mesh['dp'=4,'cp'=32] {'dp'}, dimensions={0} | all-to-all | bytes 6291456 | tf_op jit(solution)/shard_map/all_to_all | solution.py:76
  61.6 2.5 %reduce_sum.22 = bf16[128,3072]{1,0:T(8,128)(2,1)S(1)} reduce(bf16[4,128,3072]{2,1,0:T(8,128)(2,1)} %all_to_all.6, bf16[]{:T(256)} %constant.95.clone.1), dimensions={0}, to_apply=%region_0.1 | reduce | flops 1179648 | bytes 3932162 | tf_op jit(solution)/shard_map/reduce_sum | solution.py:84
  68.4 53.2 %all-gather.2.cloned.1.call-done = bf16[4096,1024]{1,0:T(8,128)(2,1)} async-done(((bf16[128,1024]{1,0:T(8,128)(2,1)}), bf16[4096,1024]{1,0:T(8,128)(2,1)}) %all-gather.2.cloned.1.call-update) | async-done | bytes 8388624 | tf_op jit(solution)/shard_map/all_gather | solution.py:138
  121.5 11.4 %copy.18 = bf16[4,1024,1024]{1,2,0:T(8,128)(2,1)} copy(bf16[4,1024,1024]{2,1,0:T(8,128)(2,1)} %bitcast.79) | data formatting | bytes 16777216 | tf_op jit(solution)/shard_map/while | solution.py:147
  133.1 40.7 %while.15 = (s32[]{:T(128)}, f32[4,4,128]{2,1,0:T(4,128)S(1)}, f32[4,4,128]{2,1,0:T(4,128)S(1)}, f32[4,4,128,128]{3,2,1,0:T(8,128)S(1)}, s32[4,1024]{1,0:T(4,128...) while((s32[]{:T(128)}, f32[4,4,128]{2,1,0:T(4,128)S(1)}, ...), condition=%wide.region_7.8_spmd, body=%wide.region_1.7_spmd.sunk | while | flops 1102057472 | bytes 38941920 | solution.py:147
  134.6 8.6 %conditional.2 = ((f32[4,4,128]{2,1,0:T(4,128)S(1)}, f32[4,4,128]{2,1,0:T(4,128)S(1)}, f32[4,4,128,128]{3,2,1,0:T(8,128)S(1)})) conditional(s32[]{:T(128)} %convert_element_type.65, (f32[4,4,128]{2,1,0:T(4,128)S(1)}, f32[4,4,128]{2,1,0:T(4,128)S(1)}, f32[4,4,128,128]{3,2,1,0:T(8,128)S(1)}) %tuple.49, (pred[128,1024]{0,1:T(8,128)(4,1)S(1)}, ...), branch_computations={%region_3.3_spmd, %region_4.6_spmd} | conditional | flops 1101533184 | bytes 38797348 | solution.py:129
  134.6 1.8 dynamic-slice_bitcast_fusion
  138.1 2.0 %fusion.2 = f32[4,4,128]{2,1,0:T(4,128)S(1)} fusion(f32[4,1024,128,4]{2,1,3,0:T(8,128)S(1)} %get-tuple-element.158, f32[4,4,128]{2,1,0:T(4,128)S(1)} %max.3, pred[128,1024]{0,1:T(8,128)(4,1)S(1)} %get-tuple-element.79), kind=kLoop, calls=%fused_computation.4 | loop fusion | flops 10483712 | bytes 8536064 | tf_op jit(solution)/shard_map/while/body/eval_jaxpr/cond/branch_1_fun/reduce_sum | solution.py:120
  140.1 3.1 %fusion.6 = f32[4,4,128,128]{3,2,1,0:T(8,128)S(1)} fusion(bf16[1024,4,128,1]{0,2,3,1:T(8,128)(2,1)S(1)} %bitcast.77, f32[4,1024,128,4]{2,1,3,0:T(8,128)S(1)} %get-tuple-element.158, f32[4,4,128]{2,1,0:T(4,128)S(1)} %max.3, pred[128,1024]{0,1:T(8,128)(4,1)S(1)} %get-tuple-element.79, f32[4,4,128,128]{3,2,1,0:T(8,128)S(1)} %get-tuple-element.84, ...), kind=kOutput, calls=%fused_computation.8 | convolution fusion | flops 547880960 | bytes 11681792 | tf_op jit(solution)/shard_map/while/body/eval_jaxpr/cond/branch_1_fun/gjtn,ngh->gjth/dot_general | solution.py:121
  144.8 8.6 %conditional.2 = ((f32[4,4,128]{2,1,0:T(4,128)S(1)}, f32[4,4,128]{2,1,0:T(4,128)S(1)}, f32[4,4,128,128]{3,2,1,0:T(8,128)S(1)})) conditional(s32[]{:T(128)} %convert_element_type.65, (f32[4,4,128]{2,1,0:T(4,128)S(1)}, f32[4,4,128]{2,1,0:T(4,128)S(1)}, f32[4,4,128,128]{3,2,1,0:T(8,128)S(1)}) %tuple.49, (pred[128,1024]{0,1:T(8,128)(4,1)S(1)}, ...), branch_computations={%region_3.3_spmd, %region_4.6_spmd} | conditional | flops 1101533184 | bytes 38797348 | solution.py:129
  144.8 1.8 dynamic-slice_bitcast_fusion
  146.7 1.5 fusion
  148.2 2.0 %fusion.2 = f32[4,4,128]{2,1,0:T(4,128)S(1)} fusion(f32[4,1024,128,4]{2,1,3,0:T(8,128)S(1)} %get-tuple-element.158, f32[4,4,128]{2,1,0:T(4,128)S(1)} %max.3, pred[128,1024]{0,1:T(8,128)(4,1)S(1)} %get-tuple-element.79), kind=kLoop, calls=%fused_computation.4 | loop fusion | flops 10483712 | bytes 8536064 | tf_op jit(solution)/shard_map/while/body/eval_jaxpr/cond/branch_1_fun/reduce_sum | solution.py:120
  150.3 3.1 %fusion.6 = f32[4,4,128,128]{3,2,1,0:T(8,128)S(1)} fusion(bf16[1024,4,128,1]{0,2,3,1:T(8,128)(2,1)S(1)} %bitcast.77, f32[4,1024,128,4]{2,1,3,0:T(8,128)S(1)} %get-tuple-element.158, f32[4,4,128]{2,1,0:T(4,128)S(1)} %max.3, pred[128,1024]{0,1:T(8,128)(4,1)S(1)} %get-tuple-element.79, f32[4,4,128,128]{3,2,1,0:T(8,128)S(1)} %get-tuple-element.84, ...), kind=kOutput, calls=%fused_computation.8 | convolution fusion | flops 547880960 | bytes 11681792 | tf_op jit(solution)/shard_map/while/body/eval_jaxpr/cond/branch_1_fun/gjtn,ngh->gjth/dot_general | solution.py:121
  154.9 8.6 %conditional.2 = ((f32[4,4,128]{2,1,0:T(4,128)S(1)}, f32[4,4,128]{2,1,0:T(4,128)S(1)}, f32[4,4,128,128]{3,2,1,0:T(8,128)S(1)})) conditional(s32[]{:T(128)} %convert_element_type.65, (f32[4,4,128]{2,1,0:T(4,128)S(1)}, f32[4,4,128]{2,1,0:T(4,128)S(1)}, f32[4,4,128,128]{3,2,1,0:T(8,128)S(1)}) %tuple.49, (pred[128,1024]{0,1:T(8,128)(4,1)S(1)}, ...), branch_computations={%region_3.3_spmd, %region_4.6_spmd} | conditional | flops 1101533184 | bytes 38797348 | solution.py:129
  154.9 1.8 dynamic-slice_bitcast_fusion
  158.4 2.0 %fusion.2 = f32[4,4,128]{2,1,0:T(4,128)S(1)} fusion(f32[4,1024,128,4]{2,1,3,0:T(8,128)S(1)} %get-tuple-element.158, f32[4,4,128]{2,1,0:T(4,128)S(1)} %max.3, pred[128,1024]{0,1:T(8,128)(4,1)S(1)} %get-tuple-element.79), kind=kLoop, calls=%fused_computation.4 | loop fusion | flops 10483712 | bytes 8536064 | tf_op jit(solution)/shard_map/while/body/eval_jaxpr/cond/branch_1_fun/reduce_sum | solution.py:120
  160.4 3.1 %fusion.6 = f32[4,4,128,128]{3,2,1,0:T(8,128)S(1)} fusion(bf16[1024,4,128,1]{0,2,3,1:T(8,128)(2,1)S(1)} %bitcast.77, f32[4,1024,128,4]{2,1,3,0:T(8,128)S(1)} %get-tuple-element.158, f32[4,4,128]{2,1,0:T(4,128)S(1)} %max.3, pred[128,1024]{0,1:T(8,128)(4,1)S(1)} %get-tuple-element.79, f32[4,4,128,128]{3,2,1,0:T(8,128)S(1)} %get-tuple-element.84, ...), kind=kOutput, calls=%fused_computation.8 | convolution fusion | flops 547880960 | bytes 11681792 | tf_op jit(solution)/shard_map/while/body/eval_jaxpr/cond/branch_1_fun/gjtn,ngh->gjth/dot_general | solution.py:121
  165.1 8.6 %conditional.2 = ((f32[4,4,128]{2,1,0:T(4,128)S(1)}, f32[4,4,128]{2,1,0:T(4,128)S(1)}, f32[4,4,128,128]{3,2,1,0:T(8,128)S(1)})) conditional(s32[]{:T(128)} %convert_element_type.65, (f32[4,4,128]{2,1,0:T(4,128)S(1)}, f32[4,4,128]{2,1,0:T(4,128)S(1)}, f32[4,4,128,128]{3,2,1,0:T(8,128)S(1)}) %tuple.49, (pred[128,1024]{0,1:T(8,128)(4,1)S(1)}, ...), branch_computations={%region_3.3_spmd, %region_4.6_spmd} | conditional | flops 1101533184 | bytes 38797348 | solution.py:129
  165.1 1.8 dynamic-slice_bitcast_fusion
  167.1 1.5 fusion
  168.6 2.0 %fusion.2 = f32[4,4,128]{2,1,0:T(4,128)S(1)} fusion(f32[4,1024,128,4]{2,1,3,0:T(8,128)S(1)} %get-tuple-element.158, f32[4,4,128]{2,1,0:T(4,128)S(1)} %max.3, pred[128,1024]{0,1:T(8,128)(4,1)S(1)} %get-tuple-element.79), kind=kLoop, calls=%fused_computation.4 | loop fusion | flops 10483712 | bytes 8536064 | tf_op jit(solution)/shard_map/while/body/eval_jaxpr/cond/branch_1_fun/reduce_sum | solution.py:120
  170.6 3.1 %fusion.6 = f32[4,4,128,128]{3,2,1,0:T(8,128)S(1)} fusion(bf16[1024,4,128,1]{0,2,3,1:T(8,128)(2,1)S(1)} %bitcast.77, f32[4,1024,128,4]{2,1,3,0:T(8,128)S(1)} %get-tuple-element.158, f32[4,4,128]{2,1,0:T(4,128)S(1)} %max.3, pred[128,1024]{0,1:T(8,128)(4,1)S(1)} %get-tuple-element.79, f32[4,4,128,128]{3,2,1,0:T(8,128)S(1)} %get-tuple-element.84, ...), kind=kOutput, calls=%fused_computation.8 | convolution fusion | flops 547880960 | bytes 11681792 | tf_op jit(solution)/shard_map/while/body/eval_jaxpr/cond/branch_1_fun/gjtn,ngh->gjth/dot_general | solution.py:121
  (70 shorter events, 17.5 us)
Async XLA Ops:
  6.5 1.2 copy-start
  6.5 115.0 %all-gather.2.cloned.1.call-start = ((), (), s32[]{:S(2)}) async-start(), calls=%async_computation.1 | async-start | bytes 8650752 | tf_op jit(solution)/shard_map/all_gather | solution.py:138
  7.8 10.8 %copy-start.2 = (s32[4,32]{1,0:T(4,128)S(1)}, s32[4,32]{1,0:T(4,128)}, u32[]{:S(2)}) copy-start(s32[4,32]{1,0:T(4,128)} %param.13) | copy-start | bytes 1540
  173.8 2.0 %copy-start.1 = (bf16[1,128,4096]{2,1,0:T(8,128)(2,1)S(1)}, bf16[1,128,4096]{2,1,0:T(8,128)(2,1)}, u32[]{:S(2)}) copy-start(bf16[1,128,4096]{2,1,0:T(8,128)(2,1)} %param.9) | copy-start | bytes 3145732
Sparse Core Ops, SparseCore 0:
  65.0 56.4 all-gather.1
where the time goes:
time: 184 us; the launch traced here: 183 us
  waiting for transfers between devices  53.2 us (29%)
  blocking collectives  39 us (21%)
  matrix products  28.4 us (15%)
  local copies, waits for them, and re-layouts  25.3 us (14%)
  other arithmetic  18.2 us (10%)
  between operations  15.4 us (8%)
  loops' own time  2.98 us (2%)
    all_gather x1, waiting for transfers between devices, local(): shard_rows = lax.all_gather(key_value, 'cp', axis=0, tiled=True)  53.2 us
    all_to_all x1, blocking collectives, local(): lax.all_to_all(packed.astype(jnp.bfloat16).reshape(groups_count * slab_co...  39 us
    dot_general x4, matrix products, compute(): jnp.einsum('gjtn,ngh->gjth', weights.astype(jnp.bfloat16), value_part, pr...  12.4 us
    while x2, local copies, waits for them, and re-layouts, local(): lax.scan(scan_step, start_state, (shard_rows.reshape(steps_count, step_ro...  11.7 us
    dot_general x1, matrix products, project(): projected = jnp.dot(input_rows, weight, preferred_element_type=jnp.float32)  9.99 us
    reduce_sum x4, other arithmetic, compute(): denom_out = denom_in * rescale + jnp.sum(weights, axis=-1)  8.07 us
    squeeze x4, local copies, waits for them, and re-layouts, local(): lax.scan(scan_step, start_state, (shard_rows.reshape(steps_count, step_ro...  7.07 us
    dot_general x4, matrix products, compute(): jnp.einsum('tgjh,ngh->gjtn', query_groups, key_part, preferred_element_ty...  5.98 us
  transfers between devices with their start and end apart: 1, of which 1 were waited for; matrix products, arithmetic and copies ran while one was open for 2% of the time, Pallas kernels for 0%

commit v1 on v0

v1 whole, which is shorter than its diff:
```python
import functools
import math

import jax
import jax.numpy as jnp
import numpy as np
from jax import lax
from jax.experimental import pallas as pl
from jax.experimental.pallas import tpu as pltpu
from jax.sharding import PartitionSpec as P

QH = 16
KVH = 4
HD = 128
D = 4096
SLAB = 128
ROPE_BASE = 500000.0
NEG = 1e30
RING = 4
BF = jnp.bfloat16
F32 = jnp.float32
SCALE2 = HD ** (-0.5) * math.log2(math.e)


def rope_tables():
    freq = ROPE_BASE ** (-np.arange(64, dtype=np.float64) * 2.0 / HD)
    freq = np.concatenate([freq, freq])[None, :]
    sign = np.where(np.arange(HD) < 64, -1.0, 1.0)[None, :]
    low = np.arange(SLAB, dtype=np.float64)[:, None] * freq
    high = np.arange(16, dtype=np.float64)[:, None] * SLAB * freq
    table = np.concatenate([np.cos(low), np.sin(low) * sign, np.cos(high), np.sin(high) * sign])
    return table.astype(np.float32)


def kernel(
    own_ref, seq_ref, ord_ref, x_hbm, w_hbm, tab_hbm, out_ref,
    xv, wv, tab, kst, vst, qst, kx, vx, qx, kbuf, vbuf, flag, qsel, mst, lst, acc, ost,
    local_sem, send_sem, flag_sem, kx_sem, vx_sem, qx_sem, kg_sem, vg_sem, out_sem,
):
    row = lax.axis_index("dp")
    cp = lax.axis_index("cp")
    core = lax.rem(cp, 2)
    chip = cp // 2
    y = lax.rem(chip, RING)
    z = chip // RING
    other = 1 - core
    first = y * other + z * core
    second = z * other + y * core

    def cp_of(first_at, second_at, which_core):
        y_at = first_at * other + second_at * core
        z_at = second_at * other + first_at * core
        return (z_at * RING + y_at) * 2 + which_core

    def x_peer(shift, which_core):
        return (lax.rem(row + shift, RING), chip * 2 + which_core)

    def plane_peer(df, ds):
        return (row, cp_of(lax.rem(first + df, RING), lax.rem(second + ds, RING), core))

    def piece_col(df, ds):
        return cp_of(lax.rem(first + df, RING), lax.rem(second + ds, RING), 0)

    sends = []

    def send(src, dst, sem, peer):
        copy = pltpu.make_async_remote_copy(
            src_ref=src, dst_ref=dst, send_sem=send_sem.at[len(sends)], recv_sem=sem,
            device_id=peer, device_id_type=pl.DeviceIdType.MESH,
        )
        copy.start()
        sends.append(copy)

    def arrived(dst, sem):
        pltpu.make_async_remote_copy(
            src_ref=dst, dst_ref=dst, send_sem=send_sem.at[0], recv_sem=sem,
            device_id=(row, cp), device_id_type=pl.DeviceIdType.MESH,
        ).wait_recv()

    barrier = pltpu.get_barrier_semaphore()
    peers = [(row, chip * 2 + other)]
    for which in (0, 1):
        peers += [x_peer(shift, which) for shift in (1, 2, 3)]
    for shift in (1, 3):
        peers += [plane_peer(shift, 0), plane_peer(0, shift)]
    for peer in peers:
        pl.semaphore_signal(barrier, inc=1, device_id=peer, device_id_type=pl.DeviceIdType.MESH)

    columns = [2048, 2560, 0, 512, 1024, 1536]
    loads = [
        pltpu.make_async_copy(w_hbm.at[:, pl.ds(c, 512)], wv.at[i], local_sem.at[i])
        for i, c in enumerate(columns)
    ]
    x_load = pltpu.make_async_copy(x_hbm, xv, local_sem.at[6])
    tab_load = pltpu.make_async_copy(tab_hbm, tab, local_sem.at[7])
    x_load.start()
    tab_load.start()
    loads[0].start()
    loads[1].start()

    target = own_ref[0, 0]
    order = ord_ref[target, cp]
    flag[0, core] = jnp.full((8, 128), target, jnp.int32)
    tab_load.wait()
    cos_low, sin_low = tab[0:128, :], tab[128:256, :]
    cos_high = tab[pl.ds(256 + order, 1), :]
    sin_high = tab[pl.ds(272 + order, 1), :]
    cosine = cos_low * cos_high - sin_low * sin_high
    lane = lax.broadcasted_iota(jnp.int32, (SLAB, HD), 1)
    sign = jnp.where(lane < 64, -1.0, 1.0).astype(F32)
    sine = (sin_low * cos_high + cos_low * sin_high)

    def rope(head):
        return (head * cosine + pltpu.roll(head, 64, 1) * sine).astype(BF)

    def project(block):
        return jnp.dot(xv[...], wv[block], preferred_element_type=F32)

    x_load.wait()
    loads[0].wait()
    loads[2].start()
    loads[3].start()
    keys = project(0)
    for h in range(2):
        for g in range(2):
            c = (h * 2 + g) * HD
            kst[h, g] = rope(keys[:, c:c + HD])
    kx[0, core] = kst[core]
    pl.semaphore_wait(barrier, len(peers))

    send(flag.at[0, core], flag.at[0, core], flag_sem.at[0, 0], (row, chip * 2 + other))
    for shift in (1, 2, 3):
        back = RING - shift
        for which in (0, 1):
            send(flag.at[0, core], flag.at[back, core], flag_sem.at[back, core], x_peer(shift, which))

    def x_send(stage, xbuf, sem):
        for which in (0, 1):
            send(stage.at[which], xbuf.at[3, core], sem.at[3, core], x_peer(1, which))
            send(stage.at[which], xbuf.at[1, core], sem.at[1, core], x_peer(3, which))
        send(stage.at[other], xbuf.at[0, core], sem.at[0, 0], (row, chip * 2 + other))

    def x_relay(xbuf, sem):
        arrived(xbuf.at[3, 0], sem.at[3, 0])
        send(xbuf.at[3, 0], xbuf.at[2, 0], sem.at[2, 0], x_peer(1, core))
        arrived(xbuf.at[1, 1], sem.at[1, 1])
        send(xbuf.at[1, 1], xbuf.at[2, 1], sem.at[2, 1], x_peer(3, core))

    def x_rest(xbuf, sem):
        arrived(xbuf.at[0, other], sem.at[0, 0])
        arrived(xbuf.at[3, 1], sem.at[3, 1])
        arrived(xbuf.at[1, 0], sem.at[1, 0])
        arrived(xbuf.at[2, 0], sem.at[2, 0])
        arrived(xbuf.at[2, 1], sem.at[2, 1])

    x_send(kst, kx, kx_sem)
    loads[1].wait()
    loads[4].start()
    values = project(1)
    for h in range(2):
        for g in range(2):
            c = (h * 2 + g) * HD
            vst[h, g] = values[:, c:c + HD].T.astype(BF)
    vx[0, core] = vst[core]
    x_send(vst, vx, vx_sem)
    loads[2].wait()
    loads[5].start()

    def query_block(i):
        block = project(2 + i)
        for j in range(4):
            qst[i // 2, i % 2, :, j * HD:(j + 1) * HD] = rope(block[:, j * HD:(j + 1) * HD])

    query_block(0)
    loads[3].wait()
    query_block(1)
    x_relay(kx, kx_sem)
    loads[4].wait()
    query_block(2)
    x_relay(vx, vx_sem)
    loads[5].wait()
    query_block(3)
    qx[0, core] = qst[core]

    arrived(flag.at[0, other], flag_sem.at[0, 0])
    for d in (1, 2, 3):
        for p in (0, 1):
            arrived(flag.at[d, p], flag_sem.at[d, p])

    def pick(parts, p):
        total = None
        for d in range(RING):
            chosen = flag[d, p, 0:1, :] == row
            part = parts(d)
            wide = jnp.broadcast_to(chosen, part.shape)
            total = jnp.where(wide, part, jnp.zeros_like(part) if total is None else total)
        return total

    my_col = chip * 2

    def gather_start(xbuf, buf, sem, gsem):
        x_rest(xbuf, sem)
        for p in (0, 1):
            for g in (0, 1):
                buf[my_col + p, g] = pick(lambda d: xbuf[d, p, g], p)

    def hop(buf, gsem, df, ds, step_f, step_s, which=None):
        col = piece_col(df, ds)
        at = (df - step_f) % RING, (ds - step_s) % RING
        slot = buf.at[pl.ds(col, 2)] if which is None else buf.at[pl.ds(col + which, 1)]
        send(slot, slot, gsem.at[at[0], at[1], which or 0], plane_peer(step_f % RING, step_s % RING))

    def landed(buf, gsem, df, ds, which=None):
        col = piece_col(df, ds)
        slot = buf.at[pl.ds(col, 2)] if which is None else buf.at[pl.ds(col + which, 1)]
        arrived(slot, gsem.at[df, ds, which or 0])

    both = ((kbuf, kg_sem), (vbuf, vg_sem))
    for xbuf, sem, (buf, gsem) in ((kx, kx_sem, both[0]), (vx, vx_sem, both[1])):
        gather_start(xbuf, buf, sem, gsem)
        hop(buf, gsem, 0, 0, 1, 0)
        hop(buf, gsem, 0, 0, -1, 0)
        hop(buf, gsem, 0, 0, 0, 1)
        hop(buf, gsem, 0, 0, 0, -1)

    x_send(qst, qx, qx_sem)

    for buf, gsem in both:
        landed(buf, gsem, 3, 0)
        hop(buf, gsem, 3, 0, 1, 0, 0)
        hop(buf, gsem, 3, 0, 0, 1)
        hop(buf, gsem, 3, 0, 0, -1)
        landed(buf, gsem, 1, 0)
        hop(buf, gsem, 1, 0, -1, 0, 1)
        hop(buf, gsem, 1, 0, 0, 1)
        hop(buf, gsem, 1, 0, 0, -1)
    x_relay(qx, qx_sem)
    for buf, gsem in both:
        landed(buf, gsem, 2, 0, 0)
        landed(buf, gsem, 2, 0, 1)
        hop(buf, gsem, 2, 0, 0, 1)
        hop(buf, gsem, 2, 0, 0, -1)
    for df in (0, 3, 1, 2):
        for buf, gsem in both:
            landed(buf, gsem, df, 3)
            hop(buf, gsem, df, 3, 0, 1, 0)
            landed(buf, gsem, df, 1)
            hop(buf, gsem, df, 1, 0, -1, 1)
    for df in range(RING):
        for buf, gsem in both:
            landed(buf, gsem, df, 2, 0)
            landed(buf, gsem, df, 2, 1)

    x_rest(qx, qx_sem)
    for p in (0, 1):
        for g in (0, 1):
            for j in range(4):
                c = j * HD
                qsel[p * 2 + g, c:c + HD, :] = pick(lambda d: qx[d, p, g, :, c:c + HD], p)

    def penalty(p, col):
        same = seq_ref[row, my_col + p] == seq_ref[row, col]
        before = ord_ref[row, col] <= ord_ref[row, my_col + p]
        return jnp.where(jnp.logical_and(same, before), 0.0, NEG).astype(F32)

    def attend(col, p, g, diagonal):
        at = p * 2 + g
        query = qsel[at]
        key = jnp.concatenate([kbuf[col, g], kbuf[col + 1, g]], axis=0)
        scores = lax.dot_general(key, query, (((1,), (1,)), ((), ())), preferred_element_type=F32)
        halves = [scores[:SLAB], scores[SLAB:]]
        shift = [penalty(p, col), penalty(p, col + 1)]
        if diagonal:
            key_at = lax.broadcasted_iota(jnp.int32, (SLAB, 4 * SLAB), 0)
            query_at = lax.rem(lax.broadcasted_iota(jnp.int32, (SLAB, 4 * SLAB), 1), SLAB)
            halves[p] = jnp.where(key_at <= query_at, halves[p], -NEG)
        peak = jnp.maximum(
            jnp.max(halves[0], axis=0, keepdims=True) - shift[0],
            jnp.max(halves[1], axis=0, keepdims=True) - shift[1],
        )
        if not diagonal:
            old = mst[at]
            peak = jnp.maximum(peak, old)
        base = peak * SCALE2
        weights = [jnp.exp2(halves[i] * SCALE2 - (base + shift[i])) for i in (0, 1)]
        total = jnp.sum(weights[0], axis=0, keepdims=True) + jnp.sum(weights[1], axis=0, keepdims=True)
        rounded = jnp.concatenate([w.astype(BF) for w in weights], axis=0)
        value = jnp.concatenate([vbuf[col, g], vbuf[col + 1, g]], axis=1)
        product = jnp.dot(value, rounded, preferred_element_type=F32)
        mst[at] = peak
        if diagonal:
            lst[at] = total
            acc[at] = product
        else:
            fade = jnp.exp2((old - peak) * SCALE2)
            lst[at] = lst[at] * fade + total
            acc[at] = acc[at] * fade + product

    for p in (0, 1):
        for g in (0, 1):
            attend(my_col, p, g, True)

    def step(i, carry):
        col = cp_of(lax.rem(first + lax.rem(i, RING), RING), lax.rem(second + i // RING, RING), 0)
        for p in (0, 1):
            for g in (0, 1):
                attend(col, p, g, False)
        return carry

    lax.fori_loop(1, RING * RING, step, 0)

    def finish(p, g):
        at = p * 2 + g
        result = acc[at] / lst[at]
        return [result[:, j * HD:(j + 1) * HD].T.astype(BF) for j in range(4)]

    for g in (0, 1):
        for j, part in enumerate(finish(other, g)):
            ost[:, (g * 4 + j) * HD:(g * 4 + j + 1) * HD] = part
    send(ost, out_ref.at[core], out_sem.at[0], (row, chip * 2 + other))
    for g in (0, 1):
        for j, part in enumerate(finish(core, g)):
            out_ref[core, :, (g * 4 + j) * HD:(g * 4 + j + 1) * HD] = part
    arrived(out_ref.at[other], out_sem.at[0])
    for copy in sends:
        copy.wait_send()


def local(tokens, qkv_weight, owner_slot, slab_sequence, slab_order):
    smem = pl.BlockSpec(memory_space=pltpu.SMEM)
    hbm = pl.BlockSpec(memory_space=pl.ANY)
    dma = pltpu.SemaphoreType.DMA
    out = pl.pallas_call(
        kernel,
        out_shape=jax.ShapeDtypeStruct((2, SLAB, QH * HD // 2), BF),
        in_specs=[smem, smem, smem, hbm, hbm, hbm],
        out_specs=pl.BlockSpec(memory_space=pltpu.VMEM),
        scratch_shapes=[
            pltpu.VMEM((SLAB, D), BF),
            pltpu.VMEM((6, D, 512), BF),
            pltpu.VMEM((288, HD), F32),
            pltpu.VMEM((2, 2, SLAB, HD), BF),
            pltpu.VMEM((2, 2, HD, SLAB), BF),
            pltpu.VMEM((2, 2, SLAB, 512), BF),
            pltpu.VMEM((4, 2, 2, SLAB, HD), BF),
            pltpu.VMEM((4, 2, 2, HD, SLAB), BF),
            pltpu.VMEM((4, 2, 2, SLAB, 512), BF),
            pltpu.VMEM((32, 2, SLAB, HD), BF),
            pltpu.VMEM((32, 2, HD, SLAB), BF),
            pltpu.VMEM((4, 2, 8, 128), jnp.int32),
            pltpu.VMEM((4, 512, HD), BF),
            pltpu.VMEM((4, 1, 512), F32),
            pltpu.VMEM((4, 1, 512), F32),
            pltpu.VMEM((4, HD, 512), F32),
            pltpu.VMEM((SLAB, 1024), BF),
            dma((8,)),
            dma((80,)),
            dma((4, 2)),
            dma((4, 2)),
            dma((4, 2)),
            dma((4, 2)),
            dma((4, 4, 2)),
            dma((4, 4, 2)),
            dma((1,)),
        ],
        compiler_params=pltpu.CompilerParams(
            collective_id=0, has_side_effects=True, vmem_limit_bytes=62 * 1024 * 1024
        ),
        name="slab_attention",
    )(owner_slot, slab_sequence, slab_order, tokens[0], qkv_weight, jnp.asarray(rope_tables()))
    return out.transpose(1, 0, 2).reshape(1, SLAB, QH * HD)


def solution(mesh):
    in_specs = (P("dp", "cp", None), P(), P("dp", "cp"), P(), P())
    out_specs = P("dp", "cp", None)
    return jax.shard_map(local, mesh=mesh, in_specs=in_specs, out_specs=out_specs, check_vma=False)
```

time: 184 us -> 76.6 us (0.42)
  the two profiles are of different devices: /device:TPU:7 before, /device:TPU:1 now
where the time goes in v1:
time: 76.6 us; the launch traced here: 76.4 us
  Pallas kernels  73.4 us (96%)
  local copies, waits for them, and re-layouts  2.32 us (3%)
    pallas_call x1, Pallas kernels, local(): pl.pallas_call(kernel, out_shape=jax.ShapeDtypeStruct((2, SLAB, QH * HD /...  73.4 us

profile of v1, /device:TPU:1, one launch (start us, length us, event | category | flops | bytes accessed | tf_op | source)
XLA Modules:
  0.0 76.4 jit_solution(12036192151831689814)
XLA Ops:
  0.7 73.4 %slab_attention.1 = bf16[2,128,1024]{2,1,0:T(8,128)(2,1)} custom-call(s32[1,1]{1,0:T(1,128)S(6)} %copy.9.own_ref, s32[4,32]{1,0:T(4,128)} %seq_ref.1, s32[4,32]{1,0:T(4,128)} %ord_ref.1, bf16[128,4096]{1,0:T(8,128)(2,1)} %bitcast.5, bf16[4096,3072]{1,0:T(8,128)(2,1)} %w_hbm.1, f32[288,128]{1,0:T(8,128)} %constant.2.clone.tab_hbm), custom_call_target="tpu_custom_call" | custom-call | tf_op jit(solution)/shard_map/slab_attention/pallas_call | solution.py:333
  74.1 1.3 %copy.7 = bf16[128,2,1024]{0,2,1:T(8,128)(2,1)S(1)} copy(bf16[128,2,1024]{2,0,1:T(8,128)(2,1)} %bitcast.3) | data formatting | bytes 1048576 | tf_op jit(solution)/shard_map/transpose | solution.py:371
  75.4 1.0 %copy.8 = bf16[1,128,2048]{2,1,0:T(8,128)(2,1)} copy(bf16[1,128,2048]{1,2,0:T(8,128)(2,1)S(1)} %bitcast.4) | data formatting | bytes 1048576 | tf_op jit(solution)/shard_map/reshape | solution.py:371

commit v2 on v1

--- a/solution.py
+++ b/solution.py
@@ -34,7 +34,7 @@
 
 def kernel(
     own_ref, seq_ref, ord_ref, x_hbm, w_hbm, tab_hbm, out_ref,
-    xv, wv, tab, kst, vst, qst, kx, vx, qx, kbuf, vbuf, flag, qsel, mst, lst, acc, ost,
+    xv, wv, tab, kst, vst, qst, kx, vx, qx, kbuf, vbuf, flag, qsel, sbuf, ost, code_ref, pick_ref,
     local_sem, send_sem, flag_sem, kx_sem, vx_sem, qx_sem, kg_sem, vg_sem, out_sem,
 ):
     row = lax.axis_index("dp")
@@ -106,9 +106,7 @@
     cos_high = tab[pl.ds(256 + order, 1), :]
     sin_high = tab[pl.ds(272 + order, 1), :]
     cosine = cos_low * cos_high - sin_low * sin_high
-    lane = lax.broadcasted_iota(jnp.int32, (SLAB, HD), 1)
-    sign = jnp.where(lane < 64, -1.0, 1.0).astype(F32)
-    sine = (sin_low * cos_high + cos_low * sin_high)
+    sine = sin_low * cos_high + cos_low * sin_high
 
     def rope(head):
         return (head * cosine + pltpu.roll(head, 64, 1) * sine).astype(BF)
@@ -174,6 +172,19 @@
     query_block(0)
     loads[3].wait()
     query_block(1)
+    my_col = chip * 2
+    for j in range(32):
+        code_ref[j] = seq_ref[row, j] * 16 + ord_ref[row, j]
+
+    def look_up(i, carry):
+        wanted = seq_ref[row, my_col + i // 16] * 16 + lax.rem(i, 16)
+        found = 0
+        for j in range(32):
+            found = jnp.where(code_ref[j] == wanted, j, found)
+        pick_ref[i // 16, lax.rem(i, 16)] = found
+        return carry
+
+    lax.fori_loop(0, 32, look_up, 0)
     x_relay(kx, kx_sem)
     loads[4].wait()
     query_block(2)
@@ -195,8 +206,6 @@
             wide = jnp.broadcast_to(chosen, part.shape)
             total = jnp.where(wide, part, jnp.zeros_like(part) if total is None else total)
         return total
-
-    my_col = chip * 2
 
     def gather_start(xbuf, buf, sem, gsem):
         x_rest(xbuf, sem)
@@ -258,70 +267,69 @@
                 c = j * HD
                 qsel[p * 2 + g, c:c + HD, :] = pick(lambda d: qx[d, p, g, :, c:c + HD], p)
 
-    def penalty(p, col):
-        same = seq_ref[row, my_col + p] == seq_ref[row, col]
-        before = ord_ref[row, col] <= ord_ref[row, my_col + p]
-        return jnp.where(jnp.logical_and(same, before), 0.0, NEG).astype(F32)
-
-    def attend(col, p, g, diagonal):
-        at = p * 2 + g
-        query = qsel[at]
-        key = jnp.concatenate([kbuf[col, g], kbuf[col + 1, g]], axis=0)
+    def scores_of(t, p, g, own, query):
+        if t == 0:
+            cols = (my_col + p, pick_ref[p, 14])
+            later = (0.0, jnp.where(own > 14, 0.0, NEG).astype(F32))
+        else:
+            cols = (pick_ref[p, 2 * t - 2], pick_ref[p, 2 * t - 1])
+            later = tuple(jnp.where(own > o, 0.0, NEG).astype(F32) for o in (2 * t - 2, 2 * t - 1))
+        key = jnp.concatenate([kbuf[cols[0], g], kbuf[cols[1], g]], axis=0)
         scores = lax.dot_general(key, query, (((1,), (1,)), ((), ())), preferred_element_type=F32)
         halves = [scores[:SLAB], scores[SLAB:]]
-        shift = [penalty(p, col), penalty(p, col + 1)]
-        if diagonal:
+        if t == 0:
             key_at = lax.broadcasted_iota(jnp.int32, (SLAB, 4 * SLAB), 0)
             query_at = lax.rem(lax.broadcasted_iota(jnp.int32, (SLAB, 4 * SLAB), 1), SLAB)
-            halves[p] = jnp.where(key_at <= query_at, halves[p], -NEG)
-        peak = jnp.maximum(
-            jnp.max(halves[0], axis=0, keepdims=True) - shift[0],
-            jnp.max(halves[1], axis=0, keepdims=True) - shift[1],
-        )
-        if not diagonal:
-            old = mst[at]
-            peak = jnp.maximum(peak, old)
-        base = peak * SCALE2
-        weights = [jnp.exp2(halves[i] * SCALE2 - (base + shift[i])) for i in (0, 1)]
-        total = jnp.sum(weights[0], axis=0, keepdims=True) + jnp.sum(weights[1], axis=0, keepdims=True)
-        rounded = jnp.concatenate([w.astype(BF) for w in weights], axis=0)
-        value = jnp.concatenate([vbuf[col, g], vbuf[col + 1, g]], axis=1)
-        product = jnp.dot(value, rounded, preferred_element_type=F32)
-        mst[at] = peak
-        if diagonal:
-            lst[at] = total
-            acc[at] = product
-        else:
-            fade = jnp.exp2((old - peak) * SCALE2)
-            lst[at] = lst[at] * fade + total
-            acc[at] = acc[at] * fade + product
-
-    for p in (0, 1):
-        for g in (0, 1):
-            attend(my_col, p, g, True)
-
-    def step(i, carry):
-        col = cp_of(lax.rem(first + lax.rem(i, RING), RING), lax.rem(second + i // RING, RING), 0)
-        for p in (0, 1):
-            for g in (0, 1):
-                attend(col, p, g, False)
+            halves[0] = jnp.where(key_at <= query_at, halves[0], -NEG)
+        return cols, later, halves
+
+    def attend(p, g):
+        own = ord_ref[row, my_col + p]
+        query = qsel[p * 2 + g]
+        peak = None
+        steps = []
+        for t in range(8):
+            cols, later, halves = scores_of(t, p, g, own, query)
+            for i in (0, 1):
+                sbuf[t, i] = halves[i]
+                top = jnp.max(halves[i].reshape(16, 8, 512), axis=0) - later[i]
+                peak = top if peak is None else jnp.maximum(peak, top)
+            steps.append((cols, later))
+        base = jnp.max(peak, axis=0, keepdims=True) * SCALE2
+        total, product = None, None
+        for t in range(8):
+            cols, later = steps[t]
+            parts = []
+            for i in (0, 1):
+                weight = jnp.exp2(sbuf[t, i] * SCALE2 - (base + later[i]))
+                part = jnp.sum(weight.reshape(16, 8, 512), axis=0)
+                total = part if total is None else total + part
+                parts.append(weight.astype(BF))
+            value = jnp.concatenate([vbuf[cols[0], g], vbuf[cols[1], g]], axis=1)
+            term = jnp.dot(value, jnp.concatenate(parts, axis=0), preferred_element_type=F32)
+            product = term if product is None else product + term
+        result = product / jnp.sum(total, axis=0, keepdims=True)
+        return [result[:, j * HD:(j + 1) * HD].T.astype(BF) for j in range(4)]
+
+    def other_side(g, carry):
+        for j, part in enumerate(attend(other, g)):
+            ost[g, :, j * HD:(j + 1) * HD] = part
         return carry
 
-    lax.fori_loop(1, RING * RING, step, 0)
-
-    def finish(p, g):
-        at = p * 2 + g
-        result = acc[at] / lst[at]
-        return [result[:, j * HD:(j + 1) * HD].T.astype(BF) for j in range(4)]
-
+    lax.fori_loop(0, 2, other_side, 0)
     for g in (0, 1):
-        for j, part in enumerate(finish(other, g)):
-            ost[:, (g * 4 + j) * HD:(g * 4 + j + 1) * HD] = part
-    send(ost, out_ref.at[core], out_sem.at[0], (row, chip * 2 + other))
+        there = out_ref.at[:, pl.ds(pl.multiple_of(core * 1024 + g * 512, 512), 512)]
+        send(ost.at[g], there, out_sem.at[g], (row, chip * 2 + other))
+
+    def own_side(g, carry):
+        parts = attend(core, g)
+        out_ref[:, pl.ds(pl.multiple_of(core * 1024 + g * 512, 512), 512)] = jnp.concatenate(parts, axis=1)
+        return carry
+
+    lax.fori_loop(0, 2, own_side, 0)
     for g in (0, 1):
-        for j, part in enumerate(finish(core, g)):
-            out_ref[core, :, (g * 4 + j) * HD:(g * 4 + j + 1) * HD] = part
-    arrived(out_ref.at[other], out_sem.at[0])
+        here = out_ref.at[:, pl.ds(pl.multiple_of(other * 1024 + g * 512, 512), 512)]
+        arrived(here, out_sem.at[g])
     for copy in sends:
         copy.wait_send()
 
@@ -332,7 +340,7 @@
     dma = pltpu.SemaphoreType.DMA
     out = pl.pallas_call(
         kernel,
-        out_shape=jax.ShapeDtypeStruct((2, SLAB, QH * HD // 2), BF),
+        out_shape=jax.ShapeDtypeStruct((SLAB, QH * HD), BF),
         in_specs=[smem, smem, smem, hbm, hbm, hbm],
         out_specs=pl.BlockSpec(memory_space=pltpu.VMEM),
         scratch_shapes=[
@@ -349,10 +357,10 @@
             pltpu.VMEM((32, 2, HD, SLAB), BF),
             pltpu.VMEM((4, 2, 8, 128), jnp.int32),
             pltpu.VMEM((4, 512, HD), BF),
-            pltpu.VMEM((4, 1, 512), F32),
-            pltpu.VMEM((4, 1, 512), F32),
-            pltpu.VMEM((4, HD, 512), F32),
-            pltpu.VMEM((SLAB, 1024), BF),
+            pltpu.VMEM((8, 2, SLAB, 512), F32),
+            pltpu.VMEM((2, SLAB, 512), BF),
+            pltpu.SMEM((32,), jnp.int32),
+            pltpu.SMEM((2, 16), jnp.int32),
             dma((8,)),
             dma((80,)),
             dma((4, 2)),
@@ -361,14 +369,14 @@
             dma((4, 2)),
             dma((4, 4, 2)),
             dma((4, 4, 2)),
-            dma((1,)),
+            dma((2,)),
         ],
         compiler_params=pltpu.CompilerParams(
             collective_id=0, has_side_effects=True, vmem_limit_bytes=62 * 1024 * 1024
         ),
         name="slab_attention",
     )(owner_slot, slab_sequence, slab_order, tokens[0], qkv_weight, jnp.asarray(rope_tables()))
-    return out.transpose(1, 0, 2).reshape(1, SLAB, QH * HD)
+    return out[None]
 
 
 def solution(mesh):

time: 76.6 us -> 57.6 us (0.75)
  Pallas kernels: 73.4 us -> 54.9 us
    pallas_call x1, Pallas kernels: 73.4 us -> 54.9 us  [local(): pl.pallas_call(kernel, out_shape=jax.ShapeDtypeStruct((SLAB, QH * HD), BF...]
    unnamed x0 -> x1, local copies, waits for them, and re-layouts: none -> 1.88 us
    transpose x1 -> x0, local copies, waits for them, and re-layouts: 1.31 us -> none  [local(): return out.transpose(1, 0, 2).reshape(1, SLAB, QH * HD)]
    reshape x1 -> x0, local copies, waits for them, and re-layouts: 1.01 us -> none  [local(): return out.transpose(1, 0, 2).reshape(1, SLAB, QH * HD)]
where the time goes in v2:
time: 57.6 us; the launch traced here: 57.4 us
  Pallas kernels  54.9 us (95%)
  local copies, waits for them, and re-layouts  1.88 us (3%)
  between operations  0.66 us (1%)
    pallas_call x1, Pallas kernels, local(): pl.pallas_call(kernel, out_shape=jax.ShapeDtypeStruct((SLAB, QH * HD), BF...  54.9 us
    unnamed x1, local copies, waits for them, and re-layouts  1.88 us

profile of v2, /device:TPU:1, one launch (start us, length us, event | category | flops | bytes accessed | tf_op | source)
XLA Modules:
  0.0 57.4 jit_solution(4072011697793100457)
XLA Ops:
  0.7 54.9 %slab_attention.1 = bf16[128,2048]{1,0:T(8,128)(2,1)} custom-call(s32[1,1]{1,0:T(1,128)S(6)} %copy.8.own_ref, s32[4,32]{1,0:T(4,128)} %seq_ref.1, s32[4,32]{1,0:T(4,128)} %ord_ref.1, bf16[128,4096]{1,0:T(8,128)(2,1)} %bitcast.3, bf16[4096,3072]{1,0:T(8,128)(2,1)} %w_hbm.1, f32[288,128]{1,0:T(8,128)} %constant.2.clone.tab_hbm), custom_call_target="tpu_custom_call" | custom-call | tf_op jit(solution)/shard_map/slab_attention/pallas_call | solution.py:341
  55.5 1.9 %copy.9 = bf16[1,128,2048]{2,1,0:T(8,128)(2,1)} copy(bf16[1,128,2048]{2,1,0:T(8,128)(2,1)} %bitcast.2) | data formatting | bytes 1048576

commit v3 on v2

v3 whole, which is shorter than its diff:
```python
import functools
import math

import jax
import jax.numpy as jnp
import numpy as np
from jax import lax
from jax.experimental import pallas as pl
from jax.experimental.pallas import tpu as pltpu
from jax.sharding import PartitionSpec as P

QH = 16
KVH = 4
HD = 128
D = 4096
SLAB = 128
ROPE_BASE = 500000.0
NEG = 1e30
RING = 4
BF = jnp.bfloat16
F32 = jnp.float32
SCALE2 = HD ** (-0.5) * math.log2(math.e)


def rope_tables():
    freq = ROPE_BASE ** (-np.arange(64, dtype=np.float64) * 2.0 / HD)
    freq = np.concatenate([freq, freq])[None, :]
    sign = np.where(np.arange(HD) < 64, -1.0, 1.0)[None, :]
    low = np.arange(SLAB, dtype=np.float64)[:, None] * freq
    high = np.arange(16, dtype=np.float64)[:, None] * SLAB * freq
    table = np.concatenate([np.cos(low), np.sin(low) * sign, np.cos(high), np.sin(high) * sign])
    return table.astype(np.float32)


def kernel(
    own_ref, seq_hbm, ord_hbm, x_hbm, w_hbm, tab_hbm, out_ref,
    seq_ref, ord_ref,
    xv, wv, tab, kst, vst, qst, kx, vx, qx, kbuf0, kbuf1, vbuf0, vbuf1, flag, qsel, sbuf, mbuf, ost, code_ref, pick_ref,
    local_sem, send_sem, flag_sem, kx_sem, vx_sem, qx_sem, kg_sem, vg_sem, out_sem,
):
    row = lax.axis_index("dp")
    cp = lax.axis_index("cp")
    core = lax.rem(cp, 2)
    chip = cp // 2
    y = lax.rem(chip, RING)
    z = chip // RING
    other = 1 - core
    first = y * other + z * core
    second = z * other + y * core

    def cp_of(first_at, second_at, which_core):
        y_at = first_at * other + second_at * core
        z_at = second_at * other + first_at * core
        return (z_at * RING + y_at) * 2 + which_core

    def x_peer(shift, which_core):
        return (lax.rem(row + shift, RING), chip * 2 + which_core)

    def plane_peer(df, ds):
        return (row, cp_of(lax.rem(first + df, RING), lax.rem(second + ds, RING), core))

    def piece_col(df, ds):
        return cp_of(lax.rem(first + df, RING), lax.rem(second + ds, RING), 0)

    sends = []

    def send(src, dst, sem, peer):
        copy = pltpu.make_async_remote_copy(
            src_ref=src, dst_ref=dst, send_sem=send_sem.at[len(sends)], recv_sem=sem,
            device_id=peer, device_id_type=pl.DeviceIdType.MESH,
        )
        copy.start()
        sends.append(copy)

    def arrived(dst, sem):
        pltpu.make_async_remote_copy(
            src_ref=dst, dst_ref=dst, send_sem=send_sem.at[0], recv_sem=sem,
            device_id=(row, cp), device_id_type=pl.DeviceIdType.MESH,
        ).wait_recv()

    columns = [2048, 2560, 0, 512, 1024, 1536]
    loads = [
        pltpu.make_async_copy(w_hbm.at[:, pl.ds(c, 512)], wv.at[i], local_sem.at[i])
        for i, c in enumerate(columns)
    ]
    x_load = pltpu.make_async_copy(x_hbm, xv, local_sem.at[6])
    tab_load = pltpu.make_async_copy(tab_hbm, tab, local_sem.at[7])
    small = [
        pltpu.make_async_copy(src, dst, local_sem.at[8 + i])
        for i, (src, dst) in enumerate(((seq_hbm, seq_ref), (ord_hbm, ord_ref)))
    ]
    for copy in small:
        copy.start()
    x_load.start()
    loads[0].start()
    tab_load.start()
    loads[1].start()

    barrier = pltpu.get_barrier_semaphore()
    peers = [(row, chip * 2 + other)]
    for which in (0, 1):
        peers += [x_peer(shift, which) for shift in (1, 2, 3)]
    for shift in (1, 3):
        peers += [plane_peer(shift, 0), plane_peer(0, shift)]
    for peer in peers:
        pl.semaphore_signal(barrier, inc=1, device_id=peer, device_id_type=pl.DeviceIdType.MESH)

    for copy in small:
        copy.wait()
    target = own_ref[0, 0]
    order = ord_ref[target, cp]
    flag[0, core] = jnp.full((8, 128), target, jnp.int32)
    tab_load.wait()
    cos_low, sin_low = tab[0:128, :], tab[128:256, :]
    cos_high = tab[pl.ds(256 + order, 1), :]
    sin_high = tab[pl.ds(272 + order, 1), :]
    cosine = cos_low * cos_high - sin_low * sin_high
    sine = sin_low * cos_high + cos_low * sin_high

    def rope(head):
        return (head * cosine + pltpu.roll(head, 64, 1) * sine).astype(BF)

    def project(block):
        return jnp.dot(xv[...], wv[block], preferred_element_type=F32)

    x_load.wait()
    loads[0].wait()
    loads[2].start()
    loads[3].start()
    keys = project(0)
    for h in range(2):
        for g in range(2):
            c = (h * 2 + g) * HD
            kst[h, g] = rope(keys[:, c:c + HD])
    kx[0, core] = kst[core]
    pl.semaphore_wait(barrier, len(peers))

    send(flag.at[0, core], flag.at[0, core], flag_sem.at[0, 0], (row, chip * 2 + other))
    for shift in (1, 2, 3):
        back = RING - shift
        for which in (0, 1):
            send(flag.at[0, core], flag.at[back, core], flag_sem.at[back, core], x_peer(shift, which))

    def x_send(stage, xbuf, sem, g, halves=(0, 1)):
        for which in halves:
            send(stage.at[which, g], xbuf.at[3, core, g], sem.at[g, 3, core], x_peer(1, which))
            send(stage.at[which, g], xbuf.at[1, core, g], sem.at[g, 1, core], x_peer(3, which))
        if 0 in halves:
            send(stage.at[other, g], xbuf.at[0, core, g], sem.at[g, 0, 0], (row, chip * 2 + other))

    def x_relay(xbuf, sem, g):
        arrived(xbuf.at[3, 0, g], sem.at[g, 3, 0])
        send(xbuf.at[3, 0, g], xbuf.at[2, 0, g], sem.at[g, 2, 0], x_peer(1, core))
        arrived(xbuf.at[1, 1, g], sem.at[g, 1, 1])
        send(xbuf.at[1, 1, g], xbuf.at[2, 1, g], sem.at[g, 2, 1], x_peer(3, core))

    def x_rest(xbuf, sem, g):
        arrived(xbuf.at[0, other, g], sem.at[g, 0, 0])
        arrived(xbuf.at[3, 1, g], sem.at[g, 3, 1])
        arrived(xbuf.at[1, 0, g], sem.at[g, 1, 0])
        arrived(xbuf.at[2, 0, g], sem.at[g, 2, 0])
        arrived(xbuf.at[2, 1, g], sem.at[g, 2, 1])

    my_col = chip * 2
    kbuf, vbuf = (kbuf0, kbuf1), (vbuf0, vbuf1)

    def query_block(i):
        block = project(2 + i)
        for j in range(4):
            qst[i // 2, i % 2, :, j * HD:(j + 1) * HD] = rope(block[:, j * HD:(j + 1) * HD])

    def look_up(i, carry):
        wanted = seq_ref[row, my_col + i // 16] * 16 + lax.rem(i, 16)
        found = 0
        for j in range(32):
            found = jnp.where(code_ref[j] == wanted, j, found)
        pick_ref[i // 16, lax.rem(i, 16)] = found
        return carry

    def flags_arrived():
        arrived(flag.at[0, other], flag_sem.at[0, 0])
        for d in (1, 2, 3):
            for p in (0, 1):
                arrived(flag.at[d, p], flag_sem.at[d, p])

    def pick(parts, p):
        total = None
        for d in range(RING):
            chosen = flag[d, p, 0:1, :] == row
            part = parts(d)
            wide = jnp.broadcast_to(chosen, part.shape)
            total = jnp.where(wide, part, jnp.zeros_like(part) if total is None else total)
        return total

    chunks = [(kx, kx_sem, kbuf, kg_sem, 0), (vx, vx_sem, vbuf, vg_sem, 0),
              (kx, kx_sem, kbuf, kg_sem, 1), (vx, vx_sem, vbuf, vg_sem, 1)]

    def slot_of(buf, g, df, ds, which):
        col = piece_col(df, ds)
        return buf[g].at[pl.ds(col, 2)] if which is None else buf[g].at[pl.ds(col + which, 1)]

    def hop(chunk, df, ds, step_f, step_s, which=None):
        _, _, buf, gsem, g = chunk
        at = (df - step_f) % RING, (ds - step_s) % RING
        slot = slot_of(buf, g, df, ds, which)
        send(slot, slot, gsem.at[g, at[0], at[1], which or 0], plane_peer(step_f % RING, step_s % RING))

    def landed(chunk, df, ds, which=None):
        _, _, buf, gsem, g = chunk
        arrived(slot_of(buf, g, df, ds, which), gsem.at[g, df, ds, which or 0])

    def begin(chunk):
        xbuf, sem, buf, gsem, g = chunk
        x_rest(xbuf, sem, g)
        for p in (0, 1):
            buf[g][my_col + p] = pick(lambda d: xbuf[d, p, g], p)
        hop(chunk, 0, 0, 1, 0)
        hop(chunk, 0, 0, -1, 0)
        hop(chunk, 0, 0, 0, 1)
        hop(chunk, 0, 0, 0, -1)

    def near(chunk):
        landed(chunk, 3, 0)
        hop(chunk, 3, 0, 1, 0, 0)
        hop(chunk, 3, 0, 0, 1)
        hop(chunk, 3, 0, 0, -1)
        landed(chunk, 1, 0)
        hop(chunk, 1, 0, -1, 0, 1)
        hop(chunk, 1, 0, 0, 1)
        hop(chunk, 1, 0, 0, -1)

    def far(chunk):
        landed(chunk, 2, 0, 0)
        landed(chunk, 2, 0, 1)
        hop(chunk, 2, 0, 0, 1)
        hop(chunk, 2, 0, 0, -1)

    def cross(chunk):
        for df in (0, 3, 1, 2):
            landed(chunk, df, 3)
            hop(chunk, df, 3, 0, 1, 0)
            landed(chunk, df, 1)
            hop(chunk, df, 1, 0, -1, 1)

    def last(chunk):
        for df in range(RING):
            landed(chunk, df, 2, 0)
            landed(chunk, df, 2, 1)

    def slabs_of(t, p, own):
        if t == 0:
            cols = (my_col + p, pick_ref[p, 14])
            later = (0.0, jnp.where(own > 14, 0.0, NEG).astype(F32))
        else:
            cols = (pick_ref[p, 2 * t - 2], pick_ref[p, 2 * t - 1])
            later = tuple(jnp.where(own > o, 0.0, NEG).astype(F32) for o in (2 * t - 2, 2 * t - 1))
        return cols, later

    def scores_of(t, p, g, own, query):
        cols, later = slabs_of(t, p, own)
        key = jnp.concatenate([kbuf[g][cols[0]], kbuf[g][cols[1]]], axis=0)
        scores = lax.dot_general(key, query, (((1,), (1,)), ((), ())), preferred_element_type=F32)
        halves = [scores[:SLAB], scores[SLAB:]]
        if t == 0:
            key_at = lax.broadcasted_iota(jnp.int32, (SLAB, 4 * SLAB), 0)
            query_at = lax.rem(lax.broadcasted_iota(jnp.int32, (SLAB, 4 * SLAB), 1), SLAB)
            halves[0] = jnp.where(key_at <= query_at, halves[0], -NEG)
        return cols, later, halves

    def first_pass(p, g, at):
        own = ord_ref[row, my_col + p]
        query = qsel[p * 2 + g]
        peak = None
        for t in range(8):
            cols, later, halves = scores_of(t, p, g, own, query)
            for i in (0, 1):
                sbuf[at, t, i] = halves[i]
                top = jnp.max(halves[i].reshape(16, 8, 512), axis=0) - later[i]
                peak = top if peak is None else jnp.maximum(peak, top)
        mbuf[at] = jnp.max(peak, axis=0, keepdims=True) * SCALE2

    def second_pass(p, g, at):
        own = ord_ref[row, my_col + p]
        base = mbuf[at]
        total, product = None, None
        for t in range(8):
            cols, later = slabs_of(t, p, own)
            parts = []
            for i in (0, 1):
                weight = jnp.exp2(sbuf[at, t, i] * SCALE2 - (base + later[i]))
                part = jnp.sum(weight.reshape(16, 8, 512), axis=0)
                total = part if total is None else total + part
                parts.append(weight.astype(BF))
            value = jnp.concatenate([vbuf[g][cols[0]], vbuf[g][cols[1]]], axis=1)
            term = jnp.dot(value, jnp.concatenate(parts, axis=0), preferred_element_type=F32)
            product = term if product is None else product + term
        result = product / jnp.sum(total, axis=0, keepdims=True)
        return jnp.concatenate([result[:, j * HD:(j + 1) * HD].T.astype(BF) for j in range(4)], axis=1)

    def columns_of(half, g):
        return pl.ds(pl.multiple_of(half * 1024 + g * 512, 512), 512)

    def give(g):
        ost[g] = second_pass(other, g, 0)
        send(ost.at[g], out_ref.at[:, columns_of(core, g)], out_sem.at[g], (row, chip * 2 + other))

    def keep(g):
        out_ref[:, columns_of(core, g)] = second_pass(core, g, 1)

    def choose_query(g):
        x_rest(qx, qx_sem, g)
        for p in (0, 1):
            for j in range(4):
                c = j * HD
                qsel[p * 2 + g, c:c + HD, :] = pick(lambda d: qx[d, p, g, :, c:c + HD], p)

    def swap_end():
        for g in (0, 1):
            arrived(out_ref.at[:, columns_of(other, g)], out_sem.at[g])

    def finish_sends():
        for copy in sends:
            copy.wait_send()

    x_send(kst, kx, kx_sem, 0)
    loads[1].wait()
    loads[4].start()
    values = project(1)
    for h in range(2):
        for g in range(2):
            c = (h * 2 + g) * HD
            vst[h, g] = values[:, c:c + HD].T.astype(BF)
    vx[0, core] = vst[core]
    x_send(vst, vx, vx_sem, 0)
    loads[2].wait()
    loads[5].start()
    query_block(0)
    x_relay(kx, kx_sem, 0)
    x_send(kst, kx, kx_sem, 1)
    loads[3].wait()
    query_block(1)
    x_relay(vx, vx_sem, 0)
    x_send(vst, vx, vx_sem, 1)
    flags_arrived()
    loads[4].wait()
    query_block(2)
    begin(chunks[0])
    x_relay(kx, kx_sem, 1)
    loads[5].wait()
    query_block(3)
    qx[0, core] = qst[core]
    begin(chunks[1])
    x_relay(vx, vx_sem, 1)
    x_send(qst, qx, qx_sem, 0)
    x_send(qst, qx, qx_sem, 1)
    near(chunks[0])
    begin(chunks[2])
    near(chunks[1])
    begin(chunks[3])
    far(chunks[0])
    near(chunks[2])
    far(chunks[1])
    near(chunks[3])
    x_relay(qx, qx_sem, 0)
    cross(chunks[0])
    far(chunks[2])
    for j in range(32):
        code_ref[j] = seq_ref[row, j] * 16 + ord_ref[row, j]
    lax.fori_loop(0, 32, look_up, 0)
    cross(chunks[1])
    far(chunks[3])
    x_relay(qx, qx_sem, 1)
    cross(chunks[2])
    choose_query(0)
    last(chunks[0])
    first_pass(other, 0, 0)
    first_pass(core, 0, 1)
    cross(chunks[3])
    last(chunks[1])
    give(0)
    keep(0)
    choose_query(1)
    last(chunks[2])

    def score_side(i, carry):
        first_pass(jnp.where(i == 0, other, core), 1, i)
        return carry

    lax.fori_loop(0, 2, score_side, 0)
    last(chunks[3])
    give(1)
    keep(1)
    swap_end()
    finish_sends()


def local(tokens, qkv_weight, owner_slot, slab_sequence, slab_order):
    hbm = pl.BlockSpec(memory_space=pltpu.HBM)
    dma = pltpu.SemaphoreType.DMA
    pin = functools.partial(pltpu.with_memory_space_constraint, memory_space=pltpu.HBM)
    out = pl.pallas_call(
        kernel,
        out_shape=jax.ShapeDtypeStruct((SLAB, QH * HD), BF),
        in_specs=[pl.BlockSpec(memory_space=pltpu.SMEM)] + [hbm] * 5,
        out_specs=pl.BlockSpec(memory_space=pltpu.VMEM),
        scratch_shapes=[
            pltpu.SMEM((4, 32), jnp.int32),
            pltpu.SMEM((4, 32), jnp.int32),
            pltpu.VMEM((SLAB, D), BF),
            pltpu.VMEM((6, D, 512), BF),
            pltpu.VMEM((288, HD), F32),
            pltpu.VMEM((2, 2, SLAB, HD), BF),
            pltpu.VMEM((2, 2, HD, SLAB), BF),
            pltpu.VMEM((2, 2, SLAB, 512), BF),
            pltpu.VMEM((4, 2, 2, SLAB, HD), BF),
            pltpu.VMEM((4, 2, 2, HD, SLAB), BF),
            pltpu.VMEM((4, 2, 2, SLAB, 512), BF),
            pltpu.VMEM((32, SLAB, HD), BF),
            pltpu.VMEM((32, SLAB, HD), BF),
            pltpu.VMEM((32, HD, SLAB), BF),
            pltpu.VMEM((32, HD, SLAB), BF),
            pltpu.VMEM((4, 2, 8, 128), jnp.int32),
            pltpu.VMEM((4, 512, HD), BF),
            pltpu.VMEM((2, 8, 2, SLAB, 512), F32),
            pltpu.VMEM((2, 1, 512), F32),
            pltpu.VMEM((2, SLAB, 512), BF),
            pltpu.SMEM((32,), jnp.int32),
            pltpu.SMEM((2, 16), jnp.int32),
            dma((10,)),
            dma((131,)),
            dma((4, 2)),
            dma((2, 4, 2)),
            dma((2, 4, 2)),
            dma((2, 4, 2)),
            dma((2, 4, 4, 2)),
            dma((2, 4, 4, 2)),
            dma((2,)),
        ],
        compiler_params=pltpu.CompilerParams(
            collective_id=0, has_side_effects=True, vmem_limit_bytes=46 * 1024 * 1024
        ),
        name="slab_attention",
    )(owner_slot, pin(slab_sequence), pin(slab_order), pin(tokens[0]), qkv_weight, pin(jnp.asarray(rope_tables())))
    return out[None]


def solution(mesh):
    in_specs = (P("dp", "cp", None), P(), P("dp", "cp"), P(), P())
    out_specs = P("dp", "cp", None)
    return jax.shard_map(local, mesh=mesh, in_specs=in_specs, out_specs=out_specs, check_vma=False)
```

time: 57.6 us -> 48.4 us (0.84)
  Pallas kernels: 54.9 us -> 46.9 us
  local copies, waits for them, and re-layouts: 1.88 us -> 0.8 us
    pallas_call x1, Pallas kernels: 54.9 us -> 46.9 us  [local(): pl.pallas_call(kernel, out_shape=jax.ShapeDtypeStruct((SLAB, QH * HD), BF...]
    unnamed x1, local copies, waits for them, and re-layouts: 1.88 us -> 0.8 us
where the time goes in v3:
time: 48.4 us; the launch traced here: 48.3 us
  Pallas kernels  46.9 us (97%)
  local copies, waits for them, and re-layouts  0.8 us (2%)
  between operations  0.66 us (1%)
    pallas_call x1, Pallas kernels, local(): pl.pallas_call(kernel, out_shape=jax.ShapeDtypeStruct((SLAB, QH * HD), BF...  46.9 us

profile of v3, /device:TPU:1, one launch (start us, length us, event | category | flops | bytes accessed | tf_op | source)
XLA Modules:
  0.0 48.3 jit_solution(13226598311563358869)
XLA Ops:
  0.7 46.9 %slab_attention.1 = bf16[128,2048]{1,0:T(8,128)(2,1)S(1)} custom-call(s32[1,1]{1,0:T(1,128)S(6)} %copy.8.own_ref, s32[4,32]{1,0:T(4,128)} %seq_hbm.1, s32[4,32]{1,0:T(4,128)} %ord_hbm.1, bf16[128,4096]{1,0:T(8,128)(2,1)} %bitcast.3, bf16[4096,3072]{1,0:T(8,128)(2,1)} %w_hbm.1, f32[288,128]{1,0:T(8,128)} %constant.2.clone.tab_hbm), custom_call_target="tpu_custom_call" | custom-call | tf_op jit(solution)/shard_map/slab_attention/pallas_call | solution.py:401
  47.5 0.8 %copy.9 = bf16[1,128,2048]{2,1,0:T(8,128)(2,1)} copy(bf16[1,128,2048]{2,1,0:T(8,128)(2,1)S(1)} %bitcast.2) | data formatting | bytes 1048576

commit v4 on v3

--- a/solution.py
+++ b/solution.py
@@ -91,10 +91,9 @@
     ]
     for copy in small:
         copy.start()
+    tab_load.start()
     x_load.start()
     loads[0].start()
-    tab_load.start()
-    loads[1].start()
 
     barrier = pltpu.get_barrier_semaphore()
     peers = [(row, chip * 2 + other)]
@@ -124,6 +123,7 @@
         return jnp.dot(xv[...], wv[block], preferred_element_type=F32)
 
     x_load.wait()
+    loads[1].start()
     loads[0].wait()
     loads[2].start()
     loads[3].start()
@@ -260,6 +260,7 @@
         cols, later = slabs_of(t, p, own)
         key = jnp.concatenate([kbuf[g][cols[0]], kbuf[g][cols[1]]], axis=0)
         scores = lax.dot_general(key, query, (((1,), (1,)), ((), ())), preferred_element_type=F32)
+        scores = scores * SCALE2
         halves = [scores[:SLAB], scores[SLAB:]]
         if t == 0:
             key_at = lax.broadcasted_iota(jnp.int32, (SLAB, 4 * SLAB), 0)
@@ -277,7 +278,7 @@
                 sbuf[at, t, i] = halves[i]
                 top = jnp.max(halves[i].reshape(16, 8, 512), axis=0) - later[i]
                 peak = top if peak is None else jnp.maximum(peak, top)
-        mbuf[at] = jnp.max(peak, axis=0, keepdims=True) * SCALE2
+        mbuf[at] = jnp.max(peak, axis=0, keepdims=True)
 
     def second_pass(p, g, at):
         own = ord_ref[row, my_col + p]
@@ -287,7 +288,7 @@
             cols, later = slabs_of(t, p, own)
             parts = []
             for i in (0, 1):
-                weight = jnp.exp2(sbuf[at, t, i] * SCALE2 - (base + later[i]))
+                weight = jnp.exp2(sbuf[at, t, i] - (base + later[i]))
                 part = jnp.sum(weight.reshape(16, 8, 512), axis=0)
                 total = part if total is None else total + part
                 parts.append(weight.astype(BF))
@@ -336,10 +337,10 @@
     loads[5].start()
     query_block(0)
     x_relay(kx, kx_sem, 0)
-    x_send(kst, kx, kx_sem, 1)
     loads[3].wait()
     query_block(1)
     x_relay(vx, vx_sem, 0)
+    x_send(kst, kx, kx_sem, 1)
     x_send(vst, vx, vx_sem, 1)
     flags_arrived()
     loads[4].wait()

time: 48.4 us -> 48.6 us (level)
  no operation moved by 1% of the time
where the time goes in v4:
time: 48.6 us; the launch traced here: 48.4 us
  Pallas kernels  47 us (97%)
  local copies, waits for them, and re-layouts  0.8 us (2%)
  between operations  0.66 us (1%)
    pallas_call x1, Pallas kernels, local(): pl.pallas_call(kernel, out_shape=jax.ShapeDtypeStruct((SLAB, QH * HD), BF...  47 us

profile of v4, /device:TPU:1, one launch (start us, length us, event | category | flops | bytes accessed | tf_op | source)
XLA Modules:
  0.0 48.4 jit_solution(11931920861456926378)
XLA Ops:
  0.7 47.0 %slab_attention.1 = bf16[128,2048]{1,0:T(8,128)(2,1)S(1)} custom-call(s32[1,1]{1,0:T(1,128)S(6)} %copy.8.own_ref, s32[4,32]{1,0:T(4,128)} %seq_hbm.1, s32[4,32]{1,0:T(4,128)} %ord_hbm.1, bf16[128,4096]{1,0:T(8,128)(2,1)} %bitcast.3, bf16[4096,3072]{1,0:T(8,128)(2,1)} %w_hbm.1, f32[288,128]{1,0:T(8,128)} %constant.2.clone.tab_hbm), custom_call_target="tpu_custom_call" | custom-call | tf_op jit(solution)/shard_map/slab_attention/pallas_call | solution.py:402
  47.7 0.8 %copy.9 = bf16[1,128,2048]{2,1,0:T(8,128)(2,1)} copy(bf16[1,128,2048]{2,1,0:T(8,128)(2,1)S(1)} %bitcast.2) | data formatting | bytes 1048576

commit v5 on v3

--- a/solution.py
+++ b/solution.py
@@ -260,6 +260,7 @@
         cols, later = slabs_of(t, p, own)
         key = jnp.concatenate([kbuf[g][cols[0]], kbuf[g][cols[1]]], axis=0)
         scores = lax.dot_general(key, query, (((1,), (1,)), ((), ())), preferred_element_type=F32)
+        scores = scores * SCALE2
         halves = [scores[:SLAB], scores[SLAB:]]
         if t == 0:
             key_at = lax.broadcasted_iota(jnp.int32, (SLAB, 4 * SLAB), 0)
@@ -277,7 +278,7 @@
                 sbuf[at, t, i] = halves[i]
                 top = jnp.max(halves[i].reshape(16, 8, 512), axis=0) - later[i]
                 peak = top if peak is None else jnp.maximum(peak, top)
-        mbuf[at] = jnp.max(peak, axis=0, keepdims=True) * SCALE2
+        mbuf[at] = jnp.max(peak, axis=0, keepdims=True)
 
     def second_pass(p, g, at):
         own = ord_ref[row, my_col + p]
@@ -287,7 +288,7 @@
             cols, later = slabs_of(t, p, own)
             parts = []
             for i in (0, 1):
-                weight = jnp.exp2(sbuf[at, t, i] * SCALE2 - (base + later[i]))
+                weight = jnp.exp2(sbuf[at, t, i] - (base + later[i]))
                 part = jnp.sum(weight.reshape(16, 8, 512), axis=0)
                 total = part if total is None else total + part
                 parts.append(weight.astype(BF))

time: 48.4 us -> 48.4 us (level)
  no operation moved by 1% of the time
where the time goes in v5:
time: 48.4 us; the launch traced here: 48.3 us
  Pallas kernels  46.8 us (97%)
  local copies, waits for them, and re-layouts  0.8 us (2%)
  between operations  0.66 us (1%)
    pallas_call x1, Pallas kernels, local(): pl.pallas_call(kernel, out_shape=jax.ShapeDtypeStruct((SLAB, QH * HD), BF...  46.8 us

profile of v5, /device:TPU:1, one launch (start us, length us, event | category | flops | bytes accessed | tf_op | source)
XLA Modules:
  0.0 48.3 jit_solution(8983293761179466530)
XLA Ops:
  0.7 46.8 %slab_attention.1 = bf16[128,2048]{1,0:T(8,128)(2,1)S(1)} custom-call(s32[1,1]{1,0:T(1,128)S(6)} %copy.8.own_ref, s32[4,32]{1,0:T(4,128)} %seq_hbm.1, s32[4,32]{1,0:T(4,128)} %ord_hbm.1, bf16[128,4096]{1,0:T(8,128)(2,1)} %bitcast.3, bf16[4096,3072]{1,0:T(8,128)(2,1)} %w_hbm.1, f32[288,128]{1,0:T(8,128)} %constant.2.clone.tab_hbm), custom_call_target="tpu_custom_call" | custom-call | tf_op jit(solution)/shard_map/slab_attention/pallas_call | solution.py:402
  47.5 0.8 %copy.9 = bf16[1,128,2048]{2,1,0:T(8,128)(2,1)} copy(bf16[1,128,2048]{2,1,0:T(8,128)(2,1)S(1)} %bitcast.2) | data formatting | bytes 1048576
